TPU v7x, 8 devices: a whole 2x2x1 slice. The times are simulated.
8 devices in a mesh: depth: 2 (over z, y), col: 2 (over x), row: 2 (over core).
Axes of the slice: x: 2, y: 2, z: 1, core: 2. Of those that a mesh axis runs over, the one named last changes fastest.
Arguments:
- a_mat: bfloat16 [12288, 12288], P('row', 'col')
- b_mat: bfloat16 [12288, 12288], P('row', 'col')
Outputs:
- output: bfloat16 [12288, 12288], P(('row', 'depth'), 'col')
All inputs are finite; a program needn't handle non-finite values.
Results may differ from a plain program's by a relative error of at most 0.001.
Values are sent between devices in bfloat16 or wider.
A program may use at most 1 GiB of HBM per device.

v0:
```python
import functools

import jax
import jax.numpy as jnp
from jax import lax
from jax.experimental import pallas as pl
from jax.experimental.pallas import tpu as pltpu
from jax.sharding import PartitionSpec as P


PIECES = ((2560, 32), (2592, 96), (0, 512), (512, 512), (1024, 512), (1536, 512), (2048, 512))
LAST_ROWS = (2688, 384)
LAST_BOXES = ((0, 384, 0, 2048), (0, 384, 2048, 4096), (0, 384, 4096, 5120), (0, 240, 5120, 6144), (240, 144, 5120, 6144))
HELD_FROM = 5120


def mm_kernel(n_blk, depth, k_off, k_len, own, with_part, meta_ref, a_ref, b_loc, b_rcv, *refs):
    if with_part:
        part_ref, refs = refs[0], refs[1:]
    out_ref, b_buf, sems = refs[-3], refs[-2], refs[-1]
    row_blk, col_blk = pl.program_id(0), pl.program_id(1)
    n_steps = pl.num_programs(0) * pl.num_programs(1)
    step = row_blk * pl.num_programs(1) + col_blk
    take_loc = meta_ref[1] == (1 if own else 0)

    def fetch(blk, slot):
        cols = pl.ds(pl.multiple_of(blk * n_blk, n_blk), n_blk)

        @pl.when(take_loc)
        def _():
            pltpu.make_async_copy(b_loc.at[pl.ds(k_off, k_len), cols], b_buf.at[slot], sems.at[slot]).start()

        @pl.when(jnp.logical_not(take_loc))
        def _():
            pltpu.make_async_copy(b_rcv.at[pl.ds(k_off, k_len), cols], b_buf.at[slot], sems.at[slot]).start()

    slot = lax.rem(step, depth)

    @pl.when(step == 0)
    def _():
        for ahead in range(depth - 1):
            fetch(ahead, ahead)

    @pl.when(step + depth - 1 < n_steps)
    def _():
        fetch(lax.rem(step + depth - 1, pl.num_programs(1)), lax.rem(step + depth - 1, depth))

    pltpu.make_async_copy(b_loc.at[pl.ds(k_off, k_len), pl.ds(0, n_blk)], b_buf.at[slot], sems.at[slot]).wait()
    prod = jnp.dot(a_ref[...], b_buf[slot], preferred_element_type=jnp.float32)
    if with_part:
        prod = part_ref[...] + prod
    out_ref[...] = prod.astype(out_ref.dtype)


def mm_call(meta, a_arr, b_loc, b_rcv, part, out_buf, *, m_blk, n_rows, a_by_layer, k_off, k_len, part_off, out_off,
            out_shape, own):
    n_side = b_loc.shape[1]
    n_blk = 512 if k_len > 4096 else 1024 if k_len > 1024 else 2048
    depth = 2
    grid = (n_rows // m_blk, n_side // n_blk)
    a_step = (b_loc.shape[0] // 2) // m_blk

    def a_map(r, c, meta_ref):
        return (meta_ref[0] * a_step + r if a_by_layer else r, 0)

    a_spec = pl.BlockSpec((m_blk, k_len), a_map, pipeline_mode=pl.Buffered(1 if n_rows == m_blk else 2))
    in_specs = [a_spec, pl.BlockSpec(memory_space=pl.ANY), pl.BlockSpec(memory_space=pl.ANY)]
    operands = [a_arr, b_loc, b_rcv]
    if part is not None:
        in_specs.append(pl.BlockSpec((m_blk, n_blk), lambda r, c, meta_ref: (part_off // m_blk + r, c)))
        operands.append(part)
    aliases = {}
    if out_buf is not None:
        in_specs.append(pl.BlockSpec(memory_space=pl.ANY))
        operands.append(out_buf)
        aliases = {len(operands): 0}
    return pl.pallas_call(
        functools.partial(mm_kernel, n_blk, depth, k_off, k_len, own, part is not None),
        out_shape=out_shape,
        grid_spec=pltpu.PrefetchScalarGridSpec(
            num_scalar_prefetch=1,
            grid=grid,
            in_specs=in_specs,
            out_specs=pl.BlockSpec((m_blk, n_blk), lambda r, c, meta_ref: (out_off // m_blk + r, c)),
            scratch_shapes=[pltpu.VMEM((depth, k_len, n_blk), jnp.bfloat16), pltpu.SemaphoreType.DMA((depth,))],
        ),
        input_output_aliases=aliases,
        cost_estimate=pl.CostEstimate(
            flops=2 * n_rows * k_len * n_side, bytes_accessed=2 * (n_rows + n_side) * k_len + 6 * n_rows * n_side, transcendentals=0
        ),
        compiler_params=pltpu.CompilerParams(
            dimension_semantics=("arbitrary", "arbitrary"), vmem_limit_bytes=(58 if m_blk > 512 else 28) * 1024 * 1024
        ),
    )(meta, *operands)


def stage_kernel(k_off, row0, meta_ref, b_loc, b_rcv, part_ref, held_ref, acc_ref, meta_out, sems):
    rows = pl.ds(k_off, held_ref.shape[0])
    part_copy = pltpu.make_async_copy(part_ref.at[pl.ds(row0, acc_ref.shape[0]), :], acc_ref, sems.at[1])
    part_copy.start()
    meta_out[0] = meta_ref[0]
    meta_out[1] = meta_ref[1]

    @pl.when(meta_ref[1] == 0)
    def _():
        pltpu.make_async_copy(b_loc.at[rows, :], held_ref, sems.at[0]).start()

    @pl.when(meta_ref[1] != 0)
    def _():
        pltpu.make_async_copy(b_rcv.at[rows, :], held_ref, sems.at[0]).start()

    pltpu.make_async_copy(b_loc.at[rows, :], held_ref, sems.at[0]).wait()
    part_copy.wait()


def tail_kernel(k_off, k_len, n_blk, depth, held_off, last, box_row, row0, meta_ref, a_ref, b_loc, b_rcv, held_ref, acc_in, *refs):
    if last:
        _, out_ref, a_buf, b_buf, o_buf, a_sem, b_sems, o_sems = refs
    else:
        acc_out, a_buf, b_buf, a_sem, b_sems = refs
    (rows, _), n_side = a_buf.shape, acc_in.shape[1]
    box_rows = pl.ds(box_row, rows)
    n_steps = n_side // n_blk
    held = held_off is not None
    a_copy = pltpu.make_async_copy(a_ref, a_buf, a_sem)
    a_copy.start()

    def cols_of(blk):
        return pl.ds(pl.multiple_of(blk * n_blk, n_blk), n_blk)

    def fetch(blk, slot):
        @pl.when(meta_ref[1] == 0)
        def _():
            pltpu.make_async_copy(b_loc.at[pl.ds(k_off, k_len), cols_of(blk)], b_buf.at[slot], b_sems.at[slot]).start()

        @pl.when(meta_ref[1] != 0)
        def _():
            pltpu.make_async_copy(b_rcv.at[pl.ds(k_off, k_len), cols_of(blk)], b_buf.at[slot], b_sems.at[slot]).start()

    def store(blk):
        return pltpu.make_async_copy(o_buf.at[:, cols_of(blk)], out_ref.at[pl.ds(row0 + box_row, rows), cols_of(blk)], o_sems.at[blk])

    if not held:
        for ahead in range(depth - 1):
            fetch(ahead, ahead)
    a_copy.wait()

    def step(blk, carry):
        cols = cols_of(blk)
        if held:
            b_val = held_ref[pl.ds(held_off, k_len), cols]
        else:
            slot = lax.rem(blk, depth)

            @pl.when(blk + depth - 1 < n_steps)
            def _():
                fetch(blk + depth - 1, lax.rem(blk + depth - 1, depth))

            pltpu.make_async_copy(b_loc.at[pl.ds(k_off, k_len), pl.ds(0, n_blk)], b_buf.at[slot], b_sems.at[slot]).wait()
            b_val = b_buf[slot]
        total = acc_in[box_rows, cols] + jnp.dot(a_buf[...], b_val, preferred_element_type=jnp.float32)
        if last:
            o_buf[:, cols] = total.astype(o_buf.dtype)
            store(blk).start()
        else:
            acc_out[box_rows, cols] = total
        return carry

    lax.fori_loop(0, n_steps, step, 0, unroll=held)
    if last:
        for blk in range(n_steps):
            store(blk).wait()


SMEM = pl.BlockSpec(memory_space=pltpu.SMEM)
VMEM = pl.BlockSpec(memory_space=pltpu.VMEM)
ANY = pl.BlockSpec(memory_space=pl.ANY)


def stage_call(meta, b_loc, b_rcv, part, row0, rows):
    side, n_side = b_loc.shape
    n_held = side - HELD_FROM
    return pl.pallas_call(
        functools.partial(stage_kernel, HELD_FROM, row0),
        out_shape=(pltpu.VMEM((n_held, n_side), jnp.bfloat16), pltpu.VMEM((rows, n_side), jnp.float32), jax.ShapeDtypeStruct((2,), jnp.int32)),
        in_specs=[SMEM, ANY, ANY, ANY],
        out_specs=(VMEM, VMEM, SMEM),
        scratch_shapes=[pltpu.SemaphoreType.DMA((2,))],
        cost_estimate=pl.CostEstimate(flops=10**9, bytes_accessed=2 * n_held * n_side + 4 * rows * n_side, transcendentals=0),
        compiler_params=pltpu.CompilerParams(vmem_limit_bytes=1024 * 1024),
        name="stage",
    )(meta, b_loc, b_rcv, part)


def tail_call(meta, a_arr, b_loc, b_rcv, held, acc, out_buf, row0, box):
    box_row, rows, k_off, k_end = box
    k_len, n_side = k_end - k_off, acc.shape[1]
    last = out_buf is not None
    held_off = k_off - HELD_FROM if k_off >= HELD_FROM else None
    n_blk, depth = (1024 if k_len <= 1024 else 512), 3
    operands = [meta, a_arr, b_loc, b_rcv, pltpu.with_memory_space_constraint(held, pltpu.VMEM), pltpu.with_memory_space_constraint(acc, pltpu.VMEM)]
    in_specs = [SMEM, ANY, ANY, ANY, VMEM, VMEM]
    b_shape = (depth, k_len, n_blk) if held_off is None else (1, 16, 128)
    scratch = [pltpu.VMEM((rows, k_len), jnp.bfloat16), pltpu.VMEM(b_shape, jnp.bfloat16)]
    sems = [pltpu.SemaphoreType.DMA, pltpu.SemaphoreType.DMA((depth,))]
    if last:
        operands.append(out_buf)
        in_specs.append(ANY)
        out_shape, out_specs, aliases = jax.ShapeDtypeStruct(out_buf.shape, out_buf.dtype), ANY, {6: 0}
        scratch += [pltpu.VMEM((rows, n_side), jnp.bfloat16)] + sems + [pltpu.SemaphoreType.DMA((n_side // n_blk,))]
    else:
        out_shape, out_specs, aliases = pltpu.VMEM(acc.shape, jnp.float32), VMEM, {5: 0}
        scratch += sems
    return pl.pallas_call(
        functools.partial(tail_kernel, k_off, k_len, n_blk, depth, held_off, last, box_row, row0),
        out_shape=out_shape,
        in_specs=in_specs,
        out_specs=out_specs,
        scratch_shapes=scratch,
        input_output_aliases=aliases,
        cost_estimate=pl.CostEstimate(flops=2 * rows * k_len * n_side, bytes_accessed=2 * k_len * n_side, transcendentals=0),
        compiler_params=pltpu.CompilerParams(vmem_limit_bytes=10 * 1024 * 1024),
    )(*operands)


def solution(mesh):
    swap = [(0, 1), (1, 0)]

    def local_mm(a_blk, b_blk):
        side = a_blk.shape[0]
        half = side // 2
        layer_idx = lax.axis_index("depth")
        row_idx = lax.axis_index("row")
        col_idx = lax.axis_index("col")
        meta = jnp.stack([layer_idx, (row_idx == col_idx).astype(jnp.int32)]).astype(jnp.int32)

        row_last, n_last = LAST_ROWS
        boxes = [(row0, rows, 0, side) for row0, rows in PIECES] + [(row_last + r, n, k0, k1) for r, n, k0, k1 in LAST_BOXES]
        moved = []
        for row0, rows, k0, k1 in boxes:
            part_a = lax.dynamic_slice(a_blk, (layer_idx * half + row0, k0), (rows, k1 - k0))
            moved.append(lax.ppermute(part_a, "col", swap))
        b_rcv = lax.ppermute(b_blk, "row", swap)

        part = mm_call(
            meta, a_blk, b_blk, b_rcv, None, None, m_blk=1024, n_rows=half, a_by_layer=True, k_off=0, k_len=side,
            part_off=0, out_off=0, out_shape=jax.ShapeDtypeStruct((half, side), jnp.float32), own=True,
        )
        out = None
        for (row0, rows), a_piece in zip(PIECES, moved):
            if row0 == PIECES[-1][0]:
                held, acc, meta = stage_call(meta, b_blk, b_rcv, part, row_last, n_last)
            out = mm_call(
                meta, a_piece, b_blk, b_rcv, part, out, m_blk=rows, n_rows=rows, a_by_layer=False, k_off=0, k_len=side,
                part_off=row0, out_off=row0, out_shape=jax.ShapeDtypeStruct((half, side), jnp.bfloat16), own=False,
            )
        for box, a_piece in zip(LAST_BOXES, moved[len(PIECES):]):
            last = box[3] == side
            res = tail_call(meta, a_piece, b_blk, b_rcv, held, acc, out if last else None, row_last, box)
            acc, out = (acc, res) if last else (res, out)
        return out

    spec_in = P("row", "col")
    spec_out = P(("row", "depth"), "col")
    return jax.shard_map(local_mm, mesh=mesh, in_specs=(spec_in, spec_in), out_specs=spec_out, check_vma=False)
```

profile of v0, /device:TPU:0, one launch (start us, length us, event | category | flops | bytes accessed | tf_op | source)
XLA Modules:
  0.0 820.2 jit_solution(15047265492359450024)
XLA Ops:
  0.0 0.8 collective-permute-start
  0.8 1.8 constant_dynamic-slice_fusion
  2.6 2.5 collective-permute-start.12
  5.1 2.3 constant_dynamic-slice_fusion.1
  7.4 0.0 collective-permute-start.11
  7.4 21.6 %constant_dynamic-slice_fusion.2 = (bf16[512,6144]{1,0:T(8,128)(2,1)}, bf16[512,6144]{1,0:T(8,128)(2,1)}, bf16[512,6144]{1,0:T(8,128)(2,1)}, bf16[512,6144]{1,0:T(8,128)(2,1)}, bf16[512,6144]{1,0:T(8,128)(2,1)}) fusion(bf16[6144,6144]{1,0:T(8,128)(2,1)} %a_ref.1, s32[]{:T(128)S(6)} %select_n.36, s32[]{:T(128)S(6)} %select_n.35, s32[]{:T(128)S(6)} %select_n.34, ...), kind=kLoop, calls=%fused_computation.2 | loop fusion | bytes 62914580 | tf_op jit(solution)/shard_map/dynamic_slice | solution.py:241
  29.0 2.0 collective-permute-start.10
  31.0 0.0 collective-permute-start.9
  31.1 0.6 pad_add_fusion.meta_ref
  31.7 1.7 constant_dynamic-slice_fusion.9
  33.4 1.9 constant_dynamic-slice_fusion.8
  35.2 2.1 constant_dynamic-slice_fusion.10
  37.3 4.0 constant_dynamic-slice_fusion.7
  41.3 68.7 %collective-permute-done.b_rcv = bf16[6144,6144]{1,0:T(8,128)(2,1)} collective-permute-done((bf16[6144,6144]{1,0:T(8,128)(2,1)}, bf16[6144,6144]{1,0:T(8,128)(2,1)}, u32[]{:S(2)}, u32[]{:S(2)}) %collective-permute-start) | collective-permute-done | bytes 75497504 | tf_op jit(solution)/shard_map/ppermute | solution.py:243
  109.9 2.8 collective-permute-start.8
  112.8 250.6 %shard_map.28.part_ref.refs_0_ = f32[3072,6144]{1,0:T(8,128)} custom-call(s32[2]{0:T(128)} %pad_add_fusion.meta_ref, bf16[6144,6144]{1,0:T(8,128)(2,1)} %a_ref.1, bf16[6144,6144]{1,0:T(8,128)(2,1)} %b_loc.27, bf16[6144,6144]{1,0:T(8,128)(2,1)} %collective-permute-done.b_rcv), custom_call_target="tpu_custom_call" | custom-call | flops 231928233984 | bytes 226492416 | tf_op jit(solution)/shard_map/pallas_call | solution.py:77
  363.4 8.4 %stage.1 = (bf16[1024,6144]{1,0:T(8,128)(2,1)S(1)}, f32[384,6144]{1,0:T(8,128)S(1)}, s32[2]{0:T(128)S(1)}) custom-call(s32[2]{0:T(128)S(1)} %copy-done, bf16[6144,6144]{1,0:T(8,128)(2,1)} %b_loc.27, bf16[6144,6144]{1,0:T(8,128)(2,1)} %collective-permute-done.b_rcv, f32[3072,6144]{1,0:T(8,128)} %shard_map.28.part_ref.refs_0_), custom_call_target="tpu_custom_call" | custom-call | flops 1000000000 | bytes 22020096 | tf_op jit(solution)/shard_map/stage/pallas_call | solution.py:183
  371.8 0.0 collective-permute-done.12.a_ref
  371.8 0.0 collective-permute-start.7
  371.8 29.2 %shard_map.32.refs_1_ = bf16[3072,6144]{1,0:T(8,128)(2,1)} custom-call(s32[2]{0:T(128)S(1)} %copy-done, bf16[32,6144]{1,0:T(8,128)(2,1)} %collective-permute-done.12.a_ref, bf16[6144,6144]{1,0:T(8,128)(2,1)} %b_loc.27, bf16[6144,6144]{1,0:T(8,128)(2,1)} %collective-permute-done.b_rcv, f32[3072,6144]{1,0:T(8,128)} %shard_map.28.part_ref.refs_0_), custom_call_target="tpu_custom_call" | custom-call | flops 2415919104 | bytes 77070336 | tf_op jit(solution)/shard_map/pallas_call | solution.py:77
  401.1 0.0 collective-permute-done.11.a_ref
  401.1 2.0 collective-permute-start.6
  403.1 29.8 %shard_map.33.refs_1_ = bf16[3072,6144]{1,0:T(8,128)(2,1)} custom-call(s32[2]{0:T(128)S(1)} %copy-done, bf16[96,6144]{1,0:T(8,128)(2,1)} %collective-permute-done.11.a_ref, bf16[6144,6144]{1,0:T(8,128)(2,1)} %b_loc.27, bf16[6144,6144]{1,0:T(8,128)(2,1)} %collective-permute-done.b_rcv, ...), custom_call_target="tpu_custom_call", output_to_operand_aliasing={{}: (5, {})} | custom-call | flops 7247757312 | bytes 80216064 | tf_op jit(solution)/shard_map/pallas_call | solution.py:77
  432.9 0.0 collective-permute-done.10.a_ref
  432.9 0.0 collective-permute-start.4
  433.0 48.6 %shard_map.34.refs_1_ = bf16[3072,6144]{1,0:T(8,128)(2,1)} custom-call(s32[2]{0:T(128)S(1)} %copy-done, bf16[512,6144]{1,0:T(8,128)(2,1)} %collective-permute-done.10.a_ref, bf16[6144,6144]{1,0:T(8,128)(2,1)} %b_loc.27, bf16[6144,6144]{1,0:T(8,128)(2,1)} %collective-permute-done.b_rcv, ...), custom_call_target="tpu_custom_call", output_to_operand_aliasing={{}: (5, {})} | custom-call | flops 38654705664 | bytes 100663296 | tf_op jit(solution)/shard_map/pallas_call | solution.py:77
  481.6 0.0 collective-permute-done.9.a_ref
  481.6 2.0 collective-permute-start.3
  483.6 48.6 %shard_map.35.refs_1_ = bf16[3072,6144]{1,0:T(8,128)(2,1)} custom-call(s32[2]{0:T(128)S(1)} %copy-done, bf16[512,6144]{1,0:T(8,128)(2,1)} %collective-permute-done.9.a_ref, bf16[6144,6144]{1,0:T(8,128)(2,1)} %b_loc.27, bf16[6144,6144]{1,0:T(8,128)(2,1)} %collective-permute-done.b_rcv, ...), custom_call_target="tpu_custom_call", output_to_operand_aliasing={{}: (5, {})} | custom-call | flops 38654705664 | bytes 100663296 | tf_op jit(solution)/shard_map/pallas_call | solution.py:77
  532.2 0.0 collective-permute-done.8.a_ref
  532.2 0.0 collective-permute-start.2
  532.2 48.6 %shard_map.36.refs_1_ = bf16[3072,6144]{1,0:T(8,128)(2,1)} custom-call(s32[2]{0:T(128)S(1)} %copy-done, bf16[512,6144]{1,0:T(8,128)(2,1)} %collective-permute-done.8.a_ref, bf16[6144,6144]{1,0:T(8,128)(2,1)} %b_loc.27, bf16[6144,6144]{1,0:T(8,128)(2,1)} %collective-permute-done.b_rcv, ...), custom_call_target="tpu_custom_call", output_to_operand_aliasing={{}: (5, {})} | custom-call | flops 38654705664 | bytes 100663296 | tf_op jit(solution)/shard_map/pallas_call | solution.py:77
  580.8 0.0 collective-permute-done.7.a_ref
  580.8 2.0 collective-permute-start.5
  582.9 48.8 %shard_map.37.refs_1_ = bf16[3072,6144]{1,0:T(8,128)(2,1)} custom-call(s32[2]{0:T(128)S(1)} %copy-done, bf16[512,6144]{1,0:T(8,128)(2,1)} %collective-permute-done.7.a_ref, bf16[6144,6144]{1,0:T(8,128)(2,1)} %b_loc.27, bf16[6144,6144]{1,0:T(8,128)(2,1)} %collective-permute-done.b_rcv, ...), custom_call_target="tpu_custom_call", output_to_operand_aliasing={{}: (5, {})} | custom-call | flops 38654705664 | bytes 100663296 | tf_op jit(solution)/shard_map/pallas_call | solution.py:77
  631.6 83.1 %collective-permute-done.6.a_ref = bf16[512,6144]{1,0:T(8,128)(2,1)} collective-permute-done((bf16[512,6144]{1,0:T(8,128)(2,1)}, bf16[512,6144]{1,0:T(8,128)(2,1)}, u32[]{:S(2)}, u32[]{:S(2)}) %collective-permute-start.6) | collective-permute-done | bytes 6291488 | tf_op jit(solution)/shard_map/ppermute | solution.py:242
  714.8 2.0 collective-permute-start.1
  716.8 48.6 %shard_map.38.refs_0_ = bf16[3072,6144]{1,0:T(8,128)(2,1)} custom-call(s32[2]{0:T(128)S(1)} %get-tuple-element.8.meta_ref, bf16[512,6144]{1,0:T(8,128)(2,1)} %collective-permute-done.6.a_ref, bf16[6144,6144]{1,0:T(8,128)(2,1)} %b_loc.27, bf16[6144,6144]{1,0:T(8,128)(2,1)} %collective-permute-done.b_rcv, ...), custom_call_target="tpu_custom_call", output_to_operand_aliasing={{}: (5, {})} | custom-call | flops 38654705664 | bytes 100663296 | tf_op jit(solution)/shard_map/pallas_call | solution.py:77
  765.4 0.0 collective-permute-done.4.a_ref
  765.4 14.4 %shard_map.29.acc_in = f32[384,6144]{1,0:T(8,128)S(1)} custom-call(s32[2]{0:T(128)S(1)} %get-tuple-element.8.meta_ref, bf16[384,2048]{1,0:T(8,128)(2,1)} %collective-permute-done.4.a_ref, bf16[6144,6144]{1,0:T(8,128)(2,1)} %b_loc.27, bf16[6144,6144]{1,0:T(8,128)(2,1)} %collective-permute-done.b_rcv, ...), custom_call_target="tpu_custom_call", output_to_operand_aliasing={{}: (5, {})} | custom-call | flops 9663676416 | bytes 25165824 | tf_op jit(solution)/shard_map/pallas_call | solution.py:214
  779.8 2.3 collective-permute-done.3.a_ref
  782.2 14.4 %shard_map.30.acc_in = f32[384,6144]{1,0:T(8,128)S(1)} custom-call(s32[2]{0:T(128)S(1)} %get-tuple-element.8.meta_ref, bf16[384,2048]{1,0:T(8,128)(2,1)} %collective-permute-done.3.a_ref, bf16[6144,6144]{1,0:T(8,128)(2,1)} %b_loc.27, bf16[6144,6144]{1,0:T(8,128)(2,1)} %collective-permute-done.b_rcv, ...), custom_call_target="tpu_custom_call", output_to_operand_aliasing={{}: (5, {})} | custom-call | flops 9663676416 | bytes 25165824 | tf_op jit(solution)/shard_map/pallas_call | solution.py:214
  796.6 2.4 collective-permute-done.2.a_ref
  799.0 8.7 %shard_map.31.acc_in = f32[384,6144]{1,0:T(8,128)S(1)} custom-call(s32[2]{0:T(128)S(1)} %get-tuple-element.8.meta_ref, bf16[384,1024]{1,0:T(8,128)(2,1)} %collective-permute-done.2.a_ref, bf16[6144,6144]{1,0:T(8,128)(2,1)} %b_loc.27, bf16[6144,6144]{1,0:T(8,128)(2,1)} %collective-permute-done.b_rcv, ...), custom_call_target="tpu_custom_call", output_to_operand_aliasing={{}: (5, {})} | custom-call | flops 4831838208 | bytes 12582912 | tf_op jit(solution)/shard_map/pallas_call | solution.py:214
  807.7 1.9 collective-permute-done.5.a_ref
  809.6 5.7 shard_map.39.refs_0_
  815.3 0.4 collective-permute-done.1.a_ref
  815.7 4.3 shard_map.40
  (2 shorter events, 0.0 us)
Async XLA Ops:
  0.0 109.9 %collective-permute-start = (bf16[6144,6144]{1,0:T(8,128)(2,1)}, bf16[6144,6144]{1,0:T(8,128)(2,1)}, u32[]{:S(2)}, u32[]{:S(2)}) collective-permute-start(bf16[6144,6144]{1,0:T(8,128)(2,1)} %b_loc.27), channel_id=1, source_target_pairs={{0,1},{1,0},{2,3},{3,2},{4,5},{5,4},{6,7},{7,6}} | collective-permute-start | bytes 226492416 | tf_op jit(solution)/shard_map/ppermute | solution.py:243
  2.6 369.2 %collective-permute-start.12 = (bf16[32,6144]{1,0:T(8,128)(2,1)}, bf16[32,6144]{1,0:T(8,128)(2,1)}, u32[]{:S(2)}, u32[]{:S(2)}) collective-permute-start(bf16[32,6144]{1,0:T(8,128)(2,1)} %constant_dynamic-slice_fusion), channel_id=1, source_target_pairs={{0,2},{2,0},{1,3},{3,1},{4,6},{6,4},{5,7},{7,5}} | collective-permute-start | bytes 1179656 | tf_op jit(solution)/shard_map/ppermute | solution.py:242
  7.4 393.6 %collective-permute-start.11 = (bf16[96,6144]{1,0:T(8,128)(2,1)}, bf16[96,6144]{1,0:T(8,128)(2,1)}, u32[]{:S(2)}, u32[]{:S(2)}) collective-permute-start(bf16[96,6144]{1,0:T(8,128)(2,1)} %constant_dynamic-slice_fusion.1), channel_id=1, source_target_pairs={{0,2},{2,0},{1,3},{3,1},{4,6},{6,4},{5,7},{7,5}} | collective-permute-start | bytes 3538952 | tf_op jit(solution)/shard_map/ppermute | solution.py:242
  29.0 403.9 %collective-permute-start.10 = (bf16[512,6144]{1,0:T(8,128)(2,1)}, bf16[512,6144]{1,0:T(8,128)(2,1)}, u32[]{:S(2)}, u32[]{:S(2)}) collective-permute-start(bf16[512,6144]{1,0:T(8,128)(2,1)} %get-tuple-element.11), channel_id=1, source_target_pairs={{0,2},{2,0},{1,3},{3,1},{4,6},{6,4},{5,7},{7,5}} | collective-permute-start | bytes 18874376 | tf_op jit(solution)/shard_map/ppermute | solution.py:242
  31.0 450.5 %collective-permute-start.9 = (bf16[512,6144]{1,0:T(8,128)(2,1)}, bf16[512,6144]{1,0:T(8,128)(2,1)}, u32[]{:S(2)}, u32[]{:S(2)}) collective-permute-start(bf16[512,6144]{1,0:T(8,128)(2,1)} %get-tuple-element.12), channel_id=1, source_target_pairs={{0,2},{2,0},{1,3},{3,1},{4,6},{6,4},{5,7},{7,5}} | collective-permute-start | bytes 18874376 | tf_op jit(solution)/shard_map/ppermute | solution.py:242
  109.9 422.2 %collective-permute-start.8 = (bf16[512,6144]{1,0:T(8,128)(2,1)}, bf16[512,6144]{1,0:T(8,128)(2,1)}, u32[]{:S(2)}, u32[]{:S(2)}) collective-permute-start(bf16[512,6144]{1,0:T(8,128)(2,1)} %get-tuple-element.13), channel_id=1, source_target_pairs={{0,2},{2,0},{1,3},{3,1},{4,6},{6,4},{5,7},{7,5}} | collective-permute-start | bytes 18874376 | tf_op jit(solution)/shard_map/ppermute | solution.py:242
  112.8 250.6 %copy-start = (s32[2]{0:T(128)S(1)}, s32[2]{0:T(128)}, u32[]{:S(2)}) copy-start(s32[2]{0:T(128)} %pad_add_fusion.meta_ref) | copy-start | bytes 28
  371.8 209.0 %collective-permute-start.7 = (bf16[512,6144]{1,0:T(8,128)(2,1)}, bf16[512,6144]{1,0:T(8,128)(2,1)}, u32[]{:S(2)}, u32[]{:S(2)}) collective-permute-start(bf16[512,6144]{1,0:T(8,128)(2,1)} %get-tuple-element.14), channel_id=1, source_target_pairs={{0,2},{2,0},{1,3},{3,1},{4,6},{6,4},{5,7},{7,5}} | collective-permute-start | bytes 18874376 | tf_op jit(solution)/shard_map/ppermute | solution.py:242
  401.1 313.7 %collective-permute-start.6 = (bf16[512,6144]{1,0:T(8,128)(2,1)}, bf16[512,6144]{1,0:T(8,128)(2,1)}, u32[]{:S(2)}, u32[]{:S(2)}) collective-permute-start(bf16[512,6144]{1,0:T(8,128)(2,1)} %get-tuple-element.15), channel_id=1, source_target_pairs={{0,2},{2,0},{1,3},{3,1},{4,6},{6,4},{5,7},{7,5}} | collective-permute-start | bytes 18874376 | tf_op jit(solution)/shard_map/ppermute | solution.py:242
  432.9 332.5 %collective-permute-start.4 = (bf16[384,2048]{1,0:T(8,128)(2,1)}, bf16[384,2048]{1,0:T(8,128)(2,1)}, u32[]{:S(2)}, u32[]{:S(2)}) collective-permute-start(bf16[384,2048]{1,0:T(8,128)(2,1)} %get-tuple-element.16), channel_id=1, source_target_pairs={{0,2},{2,0},{1,3},{3,1},{4,6},{6,4},{5,7},{7,5}} | collective-permute-start | bytes 4718600 | tf_op jit(solution)/shard_map/ppermute | solution.py:242
  481.6 300.6 %collective-permute-start.3 = (bf16[384,2048]{1,0:T(8,128)(2,1)}, bf16[384,2048]{1,0:T(8,128)(2,1)}, u32[]{:S(2)}, u32[]{:S(2)}) collective-permute-start(bf16[384,2048]{1,0:T(8,128)(2,1)} %get-tuple-element.17), channel_id=1, source_target_pairs={{0,2},{2,0},{1,3},{3,1},{4,6},{6,4},{5,7},{7,5}} | collective-permute-start | bytes 4718600 | tf_op jit(solution)/shard_map/ppermute | solution.py:242
  532.2 266.8 %collective-permute-start.2 = (bf16[384,1024]{1,0:T(8,128)(2,1)}, bf16[384,1024]{1,0:T(8,128)(2,1)}, u32[]{:S(2)}, u32[]{:S(2)}) collective-permute-start(bf16[384,1024]{1,0:T(8,128)(2,1)} %constant_dynamic-slice_fusion.10), channel_id=1, source_target_pairs={{0,2},{2,0},{1,3},{3,1},{4,6},{6,4},{5,7},{7,5}} | collective-permute-start | bytes 2359304 | tf_op jit(solution)/shard_map/ppermute | solution.py:242
  580.8 228.7 %collective-permute-start.5 = (bf16[240,1024]{1,0:T(8,128)(2,1)}, bf16[240,1024]{1,0:T(8,128)(2,1)}, u32[]{:S(2)}, u32[]{:S(2)}) collective-permute-start(bf16[240,1024]{1,0:T(8,128)(2,1)} %constant_dynamic-slice_fusion.8), channel_id=1, source_target_pairs={{0,2},{2,0},{1,3},{3,1},{4,6},{6,4},{5,7},{7,5}} | collective-permute-start | bytes 1474568 | tf_op jit(solution)/shard_map/ppermute | solution.py:242
  714.8 100.9 %collective-permute-start.1 = (bf16[144,1024]{1,0:T(8,128)(2,1)}, bf16[144,1024]{1,0:T(8,128)(2,1)}, u32[]{:S(2)}, u32[]{:S(2)}) collective-permute-start(bf16[144,1024]{1,0:T(8,128)(2,1)} %constant_dynamic-slice_fusion.9), channel_id=1, source_target_pairs={{0,2},{2,0},{1,3},{3,1},{4,6},{6,4},{5,7},{7,5}} | collective-permute-start | bytes 884744 | tf_op jit(solution)/shard_map/ppermute | solution.py:242
where the time goes:
time: 821 us; the launch traced here: 820 us
  Pallas kernels  609 us (74%)
  waiting for transfers between devices  159 us (19%)
  local copies, waits for them, and re-layouts  35.3 us (4%)
  starting transfers between devices  16.4 us (2%)
    pallas_call x8, Pallas kernels, mm_call(): pl.pallas_call(functools.partial(mm_kernel, n_blk, depth, k_off, k_len, o...  553 us
    ppermute x12, waiting for transfers between devices, local_mm(): moved.append(lax.ppermute(part_a, 'col', swap))  90.2 us
    ppermute x1, waiting for transfers between devices, local_mm(): b_rcv = lax.ppermute(b_blk, 'row', swap)  68.7 us
    pallas_call x5, Pallas kernels, tail_call(): pl.pallas_call(functools.partial(tail_kernel, k_off, k_len, n_blk, depth,...  47.5 us
    dynamic_slice x7, local copies, waits for them, and re-layouts, local_mm(): lax.dynamic_slice(a_blk, (layer_idx * half + row0, k0), (rows, k1 - k0))  35.3 us
  transfers between devices with their start and end apart: 13, of which 6 were waited for; matrix products, arithmetic and copies ran while one was open for 4% of the time, Pallas kernels for 74%

commit v1 on v0

--- a/solution.py
+++ b/solution.py
@@ -12,6 +12,7 @@
 LAST_ROWS = (2688, 384)
 LAST_BOXES = ((0, 384, 0, 2048), (0, 384, 2048, 4096), (0, 384, 4096, 5120), (0, 240, 5120, 6144), (240, 144, 5120, 6144))
 HELD_FROM = 5120
+END_COLUMNS = (1536,) * 3 + (1024, 512)
 
 
 def mm_kernel(n_blk, depth, k_off, k_len, own, with_part, meta_ref, a_ref, b_loc, b_rcv, *refs):
@@ -113,15 +114,10 @@
     part_copy.wait()
 
 
-def tail_kernel(k_off, k_len, n_blk, depth, held_off, last, box_row, row0, meta_ref, a_ref, b_loc, b_rcv, held_ref, acc_in, *refs):
-    if last:
-        _, out_ref, a_buf, b_buf, o_buf, a_sem, b_sems, o_sems = refs
-    else:
-        acc_out, a_buf, b_buf, a_sem, b_sems = refs
+def tail_kernel(k_off, k_len, n_blk, depth, box_row, meta_ref, a_ref, b_loc, b_rcv, acc_in, acc_out, a_buf, b_buf, a_sem, b_sems):
     (rows, _), n_side = a_buf.shape, acc_in.shape[1]
     box_rows = pl.ds(box_row, rows)
     n_steps = n_side // n_blk
-    held = held_off is not None
     a_copy = pltpu.make_async_copy(a_ref, a_buf, a_sem)
     a_copy.start()
 
@@ -137,39 +133,43 @@
         def _():
             pltpu.make_async_copy(b_rcv.at[pl.ds(k_off, k_len), cols_of(blk)], b_buf.at[slot], b_sems.at[slot]).start()
 
-    def store(blk):
-        return pltpu.make_async_copy(o_buf.at[:, cols_of(blk)], out_ref.at[pl.ds(row0 + box_row, rows), cols_of(blk)], o_sems.at[blk])
-
-    if not held:
-        for ahead in range(depth - 1):
-            fetch(ahead, ahead)
+    for ahead in range(depth - 1):
+        fetch(ahead, ahead)
     a_copy.wait()
 
     def step(blk, carry):
+        slot = lax.rem(blk, depth)
+
+        @pl.when(blk + depth - 1 < n_steps)
+        def _():
+            fetch(blk + depth - 1, lax.rem(blk + depth - 1, depth))
+
+        pltpu.make_async_copy(b_loc.at[pl.ds(k_off, k_len), pl.ds(0, n_blk)], b_buf.at[slot], b_sems.at[slot]).wait()
         cols = cols_of(blk)
-        if held:
-            b_val = held_ref[pl.ds(held_off, k_len), cols]
-        else:
-            slot = lax.rem(blk, depth)
-
-            @pl.when(blk + depth - 1 < n_steps)
-            def _():
-                fetch(blk + depth - 1, lax.rem(blk + depth - 1, depth))
-
-            pltpu.make_async_copy(b_loc.at[pl.ds(k_off, k_len), pl.ds(0, n_blk)], b_buf.at[slot], b_sems.at[slot]).wait()
-            b_val = b_buf[slot]
-        total = acc_in[box_rows, cols] + jnp.dot(a_buf[...], b_val, preferred_element_type=jnp.float32)
-        if last:
-            o_buf[:, cols] = total.astype(o_buf.dtype)
-            store(blk).start()
-        else:
-            acc_out[box_rows, cols] = total
+        acc_out[box_rows, cols] = acc_in[box_rows, cols] + jnp.dot(a_buf[...], b_buf[slot], preferred_element_type=jnp.float32)
         return carry
 
-    lax.fori_loop(0, n_steps, step, 0, unroll=held)
-    if last:
-        for blk in range(n_steps):
-            store(blk).wait()
+    lax.fori_loop(0, n_steps, step, 0)
+
+
+def end_kernel(held_off, n_blks, box_row, row0, a_ref, held_ref, acc_ref, _, out_ref, a_buf, o_buf, a_sem, o_sems):
+    rows, k_len = a_buf.shape
+    box_rows = pl.ds(box_row, rows)
+    a_copy = pltpu.make_async_copy(a_ref, a_buf, a_sem)
+    a_copy.start()
+    a_copy.wait()
+    stores, first = [], 0
+    for blk, n_blk in enumerate(n_blks):
+        cols = pl.ds(first, n_blk)
+        total = acc_ref[box_rows, cols] + jnp.dot(
+            a_buf[...], held_ref[pl.ds(held_off, k_len), cols], preferred_element_type=jnp.float32
+        )
+        o_buf[:, cols] = total.astype(o_buf.dtype)
+        stores.append(pltpu.make_async_copy(o_buf.at[:, cols], out_ref.at[pl.ds(row0 + box_row, rows), cols], o_sems.at[blk]))
+        stores[-1].start()
+        first += n_blk
+    for copy in stores:
+        copy.wait()
 
 
 SMEM = pl.BlockSpec(memory_space=pltpu.SMEM)
@@ -192,35 +192,45 @@
     )(meta, b_loc, b_rcv, part)
 
 
-def tail_call(meta, a_arr, b_loc, b_rcv, held, acc, out_buf, row0, box):
+def tail_call(meta, a_arr, b_loc, b_rcv, acc, box):
     box_row, rows, k_off, k_end = box
     k_len, n_side = k_end - k_off, acc.shape[1]
-    last = out_buf is not None
-    held_off = k_off - HELD_FROM if k_off >= HELD_FROM else None
     n_blk, depth = (1024 if k_len <= 1024 else 512), 3
-    operands = [meta, a_arr, b_loc, b_rcv, pltpu.with_memory_space_constraint(held, pltpu.VMEM), pltpu.with_memory_space_constraint(acc, pltpu.VMEM)]
-    in_specs = [SMEM, ANY, ANY, ANY, VMEM, VMEM]
-    b_shape = (depth, k_len, n_blk) if held_off is None else (1, 16, 128)
-    scratch = [pltpu.VMEM((rows, k_len), jnp.bfloat16), pltpu.VMEM(b_shape, jnp.bfloat16)]
-    sems = [pltpu.SemaphoreType.DMA, pltpu.SemaphoreType.DMA((depth,))]
-    if last:
-        operands.append(out_buf)
-        in_specs.append(ANY)
-        out_shape, out_specs, aliases = jax.ShapeDtypeStruct(out_buf.shape, out_buf.dtype), ANY, {6: 0}
-        scratch += [pltpu.VMEM((rows, n_side), jnp.bfloat16)] + sems + [pltpu.SemaphoreType.DMA((n_side // n_blk,))]
-    else:
-        out_shape, out_specs, aliases = pltpu.VMEM(acc.shape, jnp.float32), VMEM, {5: 0}
-        scratch += sems
-    return pl.pallas_call(
-        functools.partial(tail_kernel, k_off, k_len, n_blk, depth, held_off, last, box_row, row0),
-        out_shape=out_shape,
-        in_specs=in_specs,
-        out_specs=out_specs,
-        scratch_shapes=scratch,
-        input_output_aliases=aliases,
+    return pl.pallas_call(
+        functools.partial(tail_kernel, k_off, k_len, n_blk, depth, box_row),
+        out_shape=pltpu.VMEM(acc.shape, jnp.float32),
+        in_specs=[SMEM, ANY, ANY, ANY, VMEM],
+        out_specs=VMEM,
+        scratch_shapes=[
+            pltpu.VMEM((rows, k_len), jnp.bfloat16),
+            pltpu.VMEM((depth, k_len, n_blk), jnp.bfloat16),
+            pltpu.SemaphoreType.DMA,
+            pltpu.SemaphoreType.DMA((depth,)),
+        ],
+        input_output_aliases={4: 0},
         cost_estimate=pl.CostEstimate(flops=2 * rows * k_len * n_side, bytes_accessed=2 * k_len * n_side, transcendentals=0),
         compiler_params=pltpu.CompilerParams(vmem_limit_bytes=10 * 1024 * 1024),
-    )(*operands)
+    )(meta, a_arr, b_loc, b_rcv, pltpu.with_memory_space_constraint(acc, pltpu.VMEM))
+
+
+def end_call(a_arr, held, acc, out_buf, row0, box):
+    box_row, rows, k_off, k_end = box
+    k_len, n_side = k_end - k_off, acc.shape[1]
+    return pl.pallas_call(
+        functools.partial(end_kernel, k_off - HELD_FROM, END_COLUMNS, box_row, row0),
+        out_shape=jax.ShapeDtypeStruct(out_buf.shape, out_buf.dtype),
+        in_specs=[ANY, VMEM, VMEM, ANY],
+        out_specs=ANY,
+        scratch_shapes=[
+            pltpu.VMEM((rows, k_len), jnp.bfloat16),
+            pltpu.VMEM((rows, n_side), jnp.bfloat16),
+            pltpu.SemaphoreType.DMA,
+            pltpu.SemaphoreType.DMA((len(END_COLUMNS),)),
+        ],
+        input_output_aliases={3: 0},
+        cost_estimate=pl.CostEstimate(flops=2 * rows * k_len * n_side, bytes_accessed=2 * rows * n_side, transcendentals=0),
+        compiler_params=pltpu.CompilerParams(vmem_limit_bytes=10 * 1024 * 1024),
+    )(a_arr, pltpu.with_memory_space_constraint(held, pltpu.VMEM), pltpu.with_memory_space_constraint(acc, pltpu.VMEM), out_buf)
 
 
 def solution(mesh):
@@ -255,9 +265,10 @@
                 part_off=row0, out_off=row0, out_shape=jax.ShapeDtypeStruct((half, side), jnp.bfloat16), own=False,
             )
         for box, a_piece in zip(LAST_BOXES, moved[len(PIECES):]):
-            last = box[3] == side
-            res = tail_call(meta, a_piece, b_blk, b_rcv, held, acc, out if last else None, row_last, box)
-            acc, out = (acc, res) if last else (res, out)
+            if box[2] < HELD_FROM:
+                acc = tail_call(meta, a_piece, b_blk, b_rcv, acc, box)
+            else:
+                out = end_call(a_piece, held, acc, out, row_last, box)
         return out
 
     spec_in = P("row", "col")

time: 821 us -> 820 us (level)
    pallas_call x5 -> x3, Pallas kernels: 47.5 us -> 37.5 us  [tail_call(): pl.pallas_call(functools.partial(tail_kernel, k_off, k_len, n_blk, depth,...]
    pallas_call x0 -> x2, Pallas kernels: none -> 8.7 us  [end_call(): pl.pallas_call(functools.partial(end_kernel, k_off - HELD_FROM, END_COLUM...]
where the time goes in v1:
time: 820 us
  Pallas kernels  607 us (74%)
  waiting for transfers between devices  160 us (20%)
  local copies, waits for them, and re-layouts  35.3 us (4%)
  starting transfers between devices  16.4 us (2%)
    pallas_call x8, Pallas kernels, mm_call(): pl.pallas_call(functools.partial(mm_kernel, n_blk, depth, k_off, k_len, o...  553 us
    ppermute x12, waiting for transfers between devices, local_mm(): moved.append(lax.ppermute(part_a, 'col', swap))  90.9 us
    ppermute x1, waiting for transfers between devices, local_mm(): b_rcv = lax.ppermute(b_blk, 'row', swap)  68.7 us
    pallas_call x3, Pallas kernels, tail_call(): pl.pallas_call(functools.partial(tail_kernel, k_off, k_len, n_blk, depth,...  37.5 us
    dynamic_slice x7, local copies, waits for them, and re-layouts, local_mm(): lax.dynamic_slice(a_blk, (layer_idx * half + row0, k0), (rows, k1 - k0))  35.3 us
  transfers between devices with their start and end apart: 13, of which 6 were waited for; matrix products, arithmetic and copies ran while one was open for 4% of the time, Pallas kernels for 74%

profile of v1, /device:TPU:0, one launch (start us, length us, event | category | flops | bytes accessed | tf_op | source)
XLA Modules:
  0.0 819.6 jit_solution(17271241331656846315)
XLA Ops:
  0.0 0.8 collective-permute-start.1
  0.8 1.8 constant_dynamic-slice_fusion
  2.6 2.5 collective-permute-start.12
  5.1 2.3 constant_dynamic-slice_fusion.1
  7.4 0.0 collective-permute-start.11
  7.4 21.6 %constant_dynamic-slice_fusion.2 = (bf16[512,6144]{1,0:T(8,128)(2,1)}, bf16[512,6144]{1,0:T(8,128)(2,1)}, bf16[512,6144]{1,0:T(8,128)(2,1)}, bf16[512,6144]{1,0:T(8,128)(2,1)}, bf16[512,6144]{1,0:T(8,128)(2,1)}) fusion(bf16[6144,6144]{1,0:T(8,128)(2,1)} %a_ref.1, s32[]{:T(128)S(6)} %select_n.36, s32[]{:T(128)S(6)} %select_n.35, s32[]{:T(128)S(6)} %select_n.34, ...), kind=kLoop, calls=%fused_computation.2 | loop fusion | bytes 62914580 | tf_op jit(solution)/shard_map/dynamic_slice | solution.py:251
  29.0 2.0 collective-permute-start.10
  31.0 0.0 collective-permute-start.9
  31.1 0.6 pad_add_fusion.meta_ref
  31.7 1.7 constant_dynamic-slice_fusion.9
  33.4 1.9 constant_dynamic-slice_fusion.8
  35.2 2.1 constant_dynamic-slice_fusion.10
  37.3 4.0 constant_dynamic-slice_fusion.7
  41.3 68.7 %collective-permute-done.1.b_rcv = bf16[6144,6144]{1,0:T(8,128)(2,1)} collective-permute-done((bf16[6144,6144]{1,0:T(8,128)(2,1)}, bf16[6144,6144]{1,0:T(8,128)(2,1)}, u32[]{:S(2)}, u32[]{:S(2)}) %collective-permute-start.1) | collective-permute-done | bytes 75497504 | tf_op jit(solution)/shard_map/ppermute | solution.py:253
  109.9 2.8 collective-permute-start.8
  112.8 250.6 %shard_map.28.part_ref.refs_0_ = f32[3072,6144]{1,0:T(8,128)} custom-call(s32[2]{0:T(128)} %pad_add_fusion.meta_ref, bf16[6144,6144]{1,0:T(8,128)(2,1)} %a_ref.1, bf16[6144,6144]{1,0:T(8,128)(2,1)} %b_loc.23, bf16[6144,6144]{1,0:T(8,128)(2,1)} %collective-permute-done.1.b_rcv), custom_call_target="tpu_custom_call" | custom-call | flops 231928233984 | bytes 226492416 | tf_op jit(solution)/shard_map/pallas_call | solution.py:78
  363.4 8.4 %stage.1 = (bf16[1024,6144]{1,0:T(8,128)(2,1)S(1)}, f32[384,6144]{1,0:T(8,128)S(1)}, s32[2]{0:T(128)S(1)}) custom-call(s32[2]{0:T(128)S(1)} %copy-done, bf16[6144,6144]{1,0:T(8,128)(2,1)} %b_loc.23, bf16[6144,6144]{1,0:T(8,128)(2,1)} %collective-permute-done.1.b_rcv, f32[3072,6144]{1,0:T(8,128)} %shard_map.28.part_ref.refs_0_), custom_call_target="tpu_custom_call" | custom-call | flops 1000000000 | bytes 22020096 | tf_op jit(solution)/shard_map/stage/pallas_call | solution.py:183
  371.8 0.0 collective-permute-done.12.a_ref
  371.8 0.0 collective-permute-start.7
  371.8 29.2 %shard_map.32.refs_1_ = bf16[3072,6144]{1,0:T(8,128)(2,1)} custom-call(s32[2]{0:T(128)S(1)} %copy-done, bf16[32,6144]{1,0:T(8,128)(2,1)} %collective-permute-done.12.a_ref, bf16[6144,6144]{1,0:T(8,128)(2,1)} %b_loc.23, bf16[6144,6144]{1,0:T(8,128)(2,1)} %collective-permute-done.1.b_rcv, f32[3072,6144]{1,0:T(8,128)} %shard_map.28.part_ref.refs_0_), custom_call_target="tpu_custom_call" | custom-call | flops 2415919104 | bytes 77070336 | tf_op jit(solution)/shard_map/pallas_call | solution.py:78
  401.1 0.0 collective-permute-done.11.a_ref
  401.1 2.0 collective-permute-start.6
  403.1 29.8 %shard_map.33.refs_1_ = bf16[3072,6144]{1,0:T(8,128)(2,1)} custom-call(s32[2]{0:T(128)S(1)} %copy-done, bf16[96,6144]{1,0:T(8,128)(2,1)} %collective-permute-done.11.a_ref, bf16[6144,6144]{1,0:T(8,128)(2,1)} %b_loc.23, bf16[6144,6144]{1,0:T(8,128)(2,1)} %collective-permute-done.1.b_rcv, ...), custom_call_target="tpu_custom_call", output_to_operand_aliasing={{}: (5, {})} | custom-call | flops 7247757312 | bytes 80216064 | tf_op jit(solution)/shard_map/pallas_call | solution.py:78
  432.9 0.0 collective-permute-done.10.a_ref
  432.9 0.0 collective-permute-start.4
  433.0 48.6 %shard_map.34.refs_1_ = bf16[3072,6144]{1,0:T(8,128)(2,1)} custom-call(s32[2]{0:T(128)S(1)} %copy-done, bf16[512,6144]{1,0:T(8,128)(2,1)} %collective-permute-done.10.a_ref, bf16[6144,6144]{1,0:T(8,128)(2,1)} %b_loc.23, bf16[6144,6144]{1,0:T(8,128)(2,1)} %collective-permute-done.1.b_rcv, ...), custom_call_target="tpu_custom_call", output_to_operand_aliasing={{}: (5, {})} | custom-call | flops 38654705664 | bytes 100663296 | tf_op jit(solution)/shard_map/pallas_call | solution.py:78
  481.6 0.0 collective-permute-done.9.a_ref
  481.6 2.0 collective-permute-start.3
  483.6 48.6 %shard_map.35.refs_1_ = bf16[3072,6144]{1,0:T(8,128)(2,1)} custom-call(s32[2]{0:T(128)S(1)} %copy-done, bf16[512,6144]{1,0:T(8,128)(2,1)} %collective-permute-done.9.a_ref, bf16[6144,6144]{1,0:T(8,128)(2,1)} %b_loc.23, bf16[6144,6144]{1,0:T(8,128)(2,1)} %collective-permute-done.1.b_rcv, ...), custom_call_target="tpu_custom_call", output_to_operand_aliasing={{}: (5, {})} | custom-call | flops 38654705664 | bytes 100663296 | tf_op jit(solution)/shard_map/pallas_call | solution.py:78
  532.2 0.0 collective-permute-done.8.a_ref
  532.2 0.0 collective-permute-start.2
  532.2 48.6 %shard_map.36.refs_1_ = bf16[3072,6144]{1,0:T(8,128)(2,1)} custom-call(s32[2]{0:T(128)S(1)} %copy-done, bf16[512,6144]{1,0:T(8,128)(2,1)} %collective-permute-done.8.a_ref, bf16[6144,6144]{1,0:T(8,128)(2,1)} %b_loc.23, bf16[6144,6144]{1,0:T(8,128)(2,1)} %collective-permute-done.1.b_rcv, ...), custom_call_target="tpu_custom_call", output_to_operand_aliasing={{}: (5, {})} | custom-call | flops 38654705664 | bytes 100663296 | tf_op jit(solution)/shard_map/pallas_call | solution.py:78
  580.8 0.0 collective-permute-done.7.a_ref
  580.8 2.0 collective-permute-start.5
  582.9 48.8 %shard_map.37.refs_1_ = bf16[3072,6144]{1,0:T(8,128)(2,1)} custom-call(s32[2]{0:T(128)S(1)} %copy-done, bf16[512,6144]{1,0:T(8,128)(2,1)} %collective-permute-done.7.a_ref, bf16[6144,6144]{1,0:T(8,128)(2,1)} %b_loc.23, bf16[6144,6144]{1,0:T(8,128)(2,1)} %collective-permute-done.1.b_rcv, ...), custom_call_target="tpu_custom_call", output_to_operand_aliasing={{}: (5, {})} | custom-call | flops 38654705664 | bytes 100663296 | tf_op jit(solution)/shard_map/pallas_call | solution.py:78
  631.6 83.1 %collective-permute-done.6.a_ref = bf16[512,6144]{1,0:T(8,128)(2,1)} collective-permute-done((bf16[512,6144]{1,0:T(8,128)(2,1)}, bf16[512,6144]{1,0:T(8,128)(2,1)}, u32[]{:S(2)}, u32[]{:S(2)}) %collective-permute-start.6) | collective-permute-done | bytes 6291488 | tf_op jit(solution)/shard_map/ppermute | solution.py:252
  714.8 2.0 collective-permute-start
  716.8 48.6 %shard_map.38._ = bf16[3072,6144]{1,0:T(8,128)(2,1)} custom-call(s32[2]{0:T(128)S(1)} %get-tuple-element.9.meta_ref, bf16[512,6144]{1,0:T(8,128)(2,1)} %collective-permute-done.6.a_ref, bf16[6144,6144]{1,0:T(8,128)(2,1)} %b_loc.23, bf16[6144,6144]{1,0:T(8,128)(2,1)} %collective-permute-done.1.b_rcv, ...), custom_call_target="tpu_custom_call", output_to_operand_aliasing={{}: (5, {})} | custom-call | flops 38654705664 | bytes 100663296 | tf_op jit(solution)/shard_map/pallas_call | solution.py:78
  765.4 0.0 collective-permute-done.4.a_ref
  765.4 14.4 %shard_map.29.acc_in = f32[384,6144]{1,0:T(8,128)S(1)} custom-call(s32[2]{0:T(128)S(1)} %get-tuple-element.9.meta_ref, bf16[384,2048]{1,0:T(8,128)(2,1)} %collective-permute-done.4.a_ref, bf16[6144,6144]{1,0:T(8,128)(2,1)} %b_loc.23, bf16[6144,6144]{1,0:T(8,128)(2,1)} %collective-permute-done.1.b_rcv, ...), custom_call_target="tpu_custom_call", output_to_operand_aliasing={{}: (4, {})} | custom-call | flops 9663676416 | bytes 25165824 | tf_op jit(solution)/shard_map/pallas_call | solution.py:199
  779.8 2.3 collective-permute-done.3.a_ref
  782.2 14.4 %shard_map.30.acc_in = f32[384,6144]{1,0:T(8,128)S(1)} custom-call(s32[2]{0:T(128)S(1)} %get-tuple-element.9.meta_ref, bf16[384,2048]{1,0:T(8,128)(2,1)} %collective-permute-done.3.a_ref, bf16[6144,6144]{1,0:T(8,128)(2,1)} %b_loc.23, bf16[6144,6144]{1,0:T(8,128)(2,1)} %collective-permute-done.1.b_rcv, ...), custom_call_target="tpu_custom_call", output_to_operand_aliasing={{}: (4, {})} | custom-call | flops 9663676416 | bytes 25165824 | tf_op jit(solution)/shard_map/pallas_call | solution.py:199
  796.6 2.4 collective-permute-done.2.a_ref
  799.0 8.7 %shard_map.31.acc_ref = f32[384,6144]{1,0:T(8,128)S(1)} custom-call(s32[2]{0:T(128)S(1)} %get-tuple-element.9.meta_ref, bf16[384,1024]{1,0:T(8,128)(2,1)} %collective-permute-done.2.a_ref, bf16[6144,6144]{1,0:T(8,128)(2,1)} %b_loc.23, bf16[6144,6144]{1,0:T(8,128)(2,1)} %collective-permute-done.1.b_rcv, ...), custom_call_target="tpu_custom_call", output_to_operand_aliasing={{}: (4, {})} | custom-call | flops 4831838208 | bytes 12582912 | tf_op jit(solution)/shard_map/pallas_call | solution.py:199
  807.7 1.9 collective-permute-done.5.a_ref
  809.6 5.0 shard_map.39._
  814.6 1.1 collective-permute-done.a_ref
  815.7 3.7 shard_map.40
  (2 shorter events, 0.0 us)
Async XLA Ops:
  0.0 109.9 %collective-permute-start.1 = (bf16[6144,6144]{1,0:T(8,128)(2,1)}, bf16[6144,6144]{1,0:T(8,128)(2,1)}, u32[]{:S(2)}, u32[]{:S(2)}) collective-permute-start(bf16[6144,6144]{1,0:T(8,128)(2,1)} %b_loc.23), channel_id=1, source_target_pairs={{0,1},{1,0},{2,3},{3,2},{4,5},{5,4},{6,7},{7,6}} | collective-permute-start | bytes 226492416 | tf_op jit(solution)/shard_map/ppermute | solution.py:253
  2.6 369.2 %collective-permute-start.12 = (bf16[32,6144]{1,0:T(8,128)(2,1)}, bf16[32,6144]{1,0:T(8,128)(2,1)}, u32[]{:S(2)}, u32[]{:S(2)}) collective-permute-start(bf16[32,6144]{1,0:T(8,128)(2,1)} %constant_dynamic-slice_fusion), channel_id=1, source_target_pairs={{0,2},{2,0},{1,3},{3,1},{4,6},{6,4},{5,7},{7,5}} | collective-permute-start | bytes 1179656 | tf_op jit(solution)/shard_map/ppermute | solution.py:252
  7.4 393.6 %collective-permute-start.11 = (bf16[96,6144]{1,0:T(8,128)(2,1)}, bf16[96,6144]{1,0:T(8,128)(2,1)}, u32[]{:S(2)}, u32[]{:S(2)}) collective-permute-start(bf16[96,6144]{1,0:T(8,128)(2,1)} %constant_dynamic-slice_fusion.1), channel_id=1, source_target_pairs={{0,2},{2,0},{1,3},{3,1},{4,6},{6,4},{5,7},{7,5}} | collective-permute-start | bytes 3538952 | tf_op jit(solution)/shard_map/ppermute | solution.py:252
  29.0 403.9 %collective-permute-start.10 = (bf16[512,6144]{1,0:T(8,128)(2,1)}, bf16[512,6144]{1,0:T(8,128)(2,1)}, u32[]{:S(2)}, u32[]{:S(2)}) collective-permute-start(bf16[512,6144]{1,0:T(8,128)(2,1)} %get-tuple-element.11), channel_id=1, source_target_pairs={{0,2},{2,0},{1,3},{3,1},{4,6},{6,4},{5,7},{7,5}} | collective-permute-start | bytes 18874376 | tf_op jit(solution)/shard_map/ppermute | solution.py:252
  31.0 450.5 %collective-permute-start.9 = (bf16[512,6144]{1,0:T(8,128)(2,1)}, bf16[512,6144]{1,0:T(8,128)(2,1)}, u32[]{:S(2)}, u32[]{:S(2)}) collective-permute-start(bf16[512,6144]{1,0:T(8,128)(2,1)} %get-tuple-element.12), channel_id=1, source_target_pairs={{0,2},{2,0},{1,3},{3,1},{4,6},{6,4},{5,7},{7,5}} | collective-permute-start | bytes 18874376 | tf_op jit(solution)/shard_map/ppermute | solution.py:252
  109.9 422.2 %collective-permute-start.8 = (bf16[512,6144]{1,0:T(8,128)(2,1)}, bf16[512,6144]{1,0:T(8,128)(2,1)}, u32[]{:S(2)}, u32[]{:S(2)}) collective-permute-start(bf16[512,6144]{1,0:T(8,128)(2,1)} %get-tuple-element.13), channel_id=1, source_target_pairs={{0,2},{2,0},{1,3},{3,1},{4,6},{6,4},{5,7},{7,5}} | collective-permute-start | bytes 18874376 | tf_op jit(solution)/shard_map/ppermute | solution.py:252
  112.8 250.6 %copy-start = (s32[2]{0:T(128)S(1)}, s32[2]{0:T(128)}, u32[]{:S(2)}) copy-start(s32[2]{0:T(128)} %pad_add_fusion.meta_ref) | copy-start | bytes 28
  371.8 209.0 %collective-permute-start.7 = (bf16[512,6144]{1,0:T(8,128)(2,1)}, bf16[512,6144]{1,0:T(8,128)(2,1)}, u32[]{:S(2)}, u32[]{:S(2)}) collective-permute-start(bf16[512,6144]{1,0:T(8,128)(2,1)} %get-tuple-element.14), channel_id=1, source_target_pairs={{0,2},{2,0},{1,3},{3,1},{4,6},{6,4},{5,7},{7,5}} | collective-permute-start | bytes 18874376 | tf_op jit(solution)/shard_map/ppermute | solution.py:252
  401.1 313.7 %collective-permute-start.6 = (bf16[512,6144]{1,0:T(8,128)(2,1)}, bf16[512,6144]{1,0:T(8,128)(2,1)}, u32[]{:S(2)}, u32[]{:S(2)}) collective-permute-start(bf16[512,6144]{1,0:T(8,128)(2,1)} %get-tuple-element.15), channel_id=1, source_target_pairs={{0,2},{2,0},{1,3},{3,1},{4,6},{6,4},{5,7},{7,5}} | collective-permute-start | bytes 18874376 | tf_op jit(solution)/shard_map/ppermute | solution.py:252
  432.9 332.5 %collective-permute-start.4 = (bf16[384,2048]{1,0:T(8,128)(2,1)}, bf16[384,2048]{1,0:T(8,128)(2,1)}, u32[]{:S(2)}, u32[]{:S(2)}) collective-permute-start(bf16[384,2048]{1,0:T(8,128)(2,1)} %get-tuple-element.16), channel_id=1, source_target_pairs={{0,2},{2,0},{1,3},{3,1},{4,6},{6,4},{5,7},{7,5}} | collective-permute-start | bytes 4718600 | tf_op jit(solution)/shard_map/ppermute | solution.py:252
  481.6 300.6 %collective-permute-start.3 = (bf16[384,2048]{1,0:T(8,128)(2,1)}, bf16[384,2048]{1,0:T(8,128)(2,1)}, u32[]{:S(2)}, u32[]{:S(2)}) collective-permute-start(bf16[384,2048]{1,0:T(8,128)(2,1)} %get-tuple-element.17), channel_id=1, source_target_pairs={{0,2},{2,0},{1,3},{3,1},{4,6},{6,4},{5,7},{7,5}} | collective-permute-start | bytes 4718600 | tf_op jit(solution)/shard_map/ppermute | solution.py:252
  532.2 266.8 %collective-permute-start.2 = (bf16[384,1024]{1,0:T(8,128)(2,1)}, bf16[384,1024]{1,0:T(8,128)(2,1)}, u32[]{:S(2)}, u32[]{:S(2)}) collective-permute-start(bf16[384,1024]{1,0:T(8,128)(2,1)} %constant_dynamic-slice_fusion.10), channel_id=1, source_target_pairs={{0,2},{2,0},{1,3},{3,1},{4,6},{6,4},{5,7},{7,5}} | collective-permute-start | bytes 2359304 | tf_op jit(solution)/shard_map/ppermute | solution.py:252
  580.8 228.7 %collective-permute-start.5 = (bf16[240,1024]{1,0:T(8,128)(2,1)}, bf16[240,1024]{1,0:T(8,128)(2,1)}, u32[]{:S(2)}, u32[]{:S(2)}) collective-permute-start(bf16[240,1024]{1,0:T(8,128)(2,1)} %constant_dynamic-slice_fusion.8), channel_id=1, source_target_pairs={{0,2},{2,0},{1,3},{3,1},{4,6},{6,4},{5,7},{7,5}} | collective-permute-start | bytes 1474568 | tf_op jit(solution)/shard_map/ppermute | solution.py:252
  714.8 100.9 %collective-permute-start = (bf16[144,1024]{1,0:T(8,128)(2,1)}, bf16[144,1024]{1,0:T(8,128)(2,1)}, u32[]{:S(2)}, u32[]{:S(2)}) collective-permute-start(bf16[144,1024]{1,0:T(8,128)(2,1)} %constant_dynamic-slice_fusion.9), channel_id=1, source_target_pairs={{0,2},{2,0},{1,3},{3,1},{4,6},{6,4},{5,7},{7,5}} | collective-permute-start | bytes 884744 | tf_op jit(solution)/shard_map/ppermute | solution.py:252

commit v2 on v1

--- a/solution.py
+++ b/solution.py
@@ -10,7 +10,15 @@
 
 PIECES = ((2560, 32), (2592, 96), (0, 512), (512, 512), (1024, 512), (1536, 512), (2048, 512))
 LAST_ROWS = (2688, 384)
-LAST_BOXES = ((0, 384, 0, 2048), (0, 384, 2048, 4096), (0, 384, 4096, 5120), (0, 240, 5120, 6144), (240, 144, 5120, 6144))
+LAST_BOXES = (
+    (0, 384, 0, 2048),
+    (0, 384, 2048, 3584),
+    (0, 384, 3584, 4608),
+    (0, 384, 4608, 5120),
+    (0, 176, 5120, 6144),
+    (176, 112, 5120, 6144),
+    (288, 96, 5120, 6144),
+)
 HELD_FROM = 5120
 END_COLUMNS = (1536,) * 3 + (1024, 512)
 

time: 820 us -> 821 us (level)
  waiting for transfers between devices: 160 us -> 147 us
    ppermute x12 -> x14, waiting for transfers between devices: 90.9 us -> 83.3 us  [local_mm(): moved.append(lax.ppermute(part_a, 'col', swap))]
    dynamic_slice x7 -> x10, local copies, waits for them, and re-layouts: 35.3 us -> 39.8 us  [local_mm(): lax.dynamic_slice(a_blk, (layer_idx * half + row0, k0), (rows, k1 - k0))]
    pallas_call x3 -> x4, Pallas kernels: 37.5 us -> 40.9 us  [tail_call(): pl.pallas_call(functools.partial(tail_kernel, k_off, k_len, n_blk, depth,...]
    ppermute x12 -> x14, starting transfers between devices: 15.6 us -> 17.6 us  [local_mm(): moved.append(lax.ppermute(part_a, 'col', swap))]
  transfers between devices with their start and end apart: 13 -> 15, of which waited for: 6 -> 2; matrix products, arithmetic and copies ran while one was open for 4% -> 5% of each run, Pallas kernels for 74% -> 74%
where the time goes in v2:
time: 821 us; the launch traced here: 820 us
  Pallas kernels  613 us (75%)
  waiting for transfers between devices  147 us (18%)
  local copies, waits for them, and re-layouts  39.8 us (5%)
  starting transfers between devices  18.5 us (2%)
    pallas_call x8, Pallas kernels, mm_call(): pl.pallas_call(functools.partial(mm_kernel, n_blk, depth, k_off, k_len, o...  553 us
    ppermute x14, waiting for transfers between devices, local_mm(): moved.append(lax.ppermute(part_a, 'col', swap))  83.3 us
    ppermute x1, waiting for transfers between devices, local_mm(): b_rcv = lax.ppermute(b_blk, 'row', swap)  64.2 us
    pallas_call x4, Pallas kernels, tail_call(): pl.pallas_call(functools.partial(tail_kernel, k_off, k_len, n_blk, depth,...  40.9 us
    dynamic_slice x10, local copies, waits for them, and re-layouts, local_mm(): lax.dynamic_slice(a_blk, (layer_idx * half + row0, k0), (rows, k1 - k0))  39.8 us
    ppermute x14, starting transfers between devices, local_mm(): moved.append(lax.ppermute(part_a, 'col', swap))  17.6 us
  transfers between devices with their start and end apart: 15, of which 2 were waited for; matrix products, arithmetic and copies ran while one was open for 5% of the time, Pallas kernels for 74%

profile of v2, /device:TPU:0, one launch (start us, length us, event | category | flops | bytes accessed | tf_op | source)
XLA Modules:
  0.0 820.1 jit_solution(1526459512385833205)
XLA Ops:
  0.0 0.8 collective-permute-start.1
  0.8 1.8 constant_dynamic-slice_fusion
  2.6 2.5 collective-permute-start.14
  5.1 2.4 constant_dynamic-slice_fusion.1
  7.4 0.0 collective-permute-start.13
  7.4 21.7 %constant_dynamic-slice_fusion.2 = (bf16[512,6144]{1,0:T(8,128)(2,1)}, bf16[512,6144]{1,0:T(8,128)(2,1)}, bf16[512,6144]{1,0:T(8,128)(2,1)}, bf16[512,6144]{1,0:T(8,128)(2,1)}, bf16[512,6144]{1,0:T(8,128)(2,1)}) fusion(bf16[6144,6144]{1,0:T(8,128)(2,1)} %a_ref.1, s32[]{:T(128)S(6)} %select_n.41, s32[]{:T(128)S(6)} %select_n.40, s32[]{:T(128)S(6)} %select_n.39, ...), kind=kLoop, calls=%fused_computation.2 | loop fusion | bytes 62914580 | tf_op jit(solution)/shard_map/dynamic_slice | solution.py:259
  29.1 2.0 collective-permute-start.12
  31.1 0.0 collective-permute-start.11
  31.2 0.6 pad_add_fusion.meta_ref
  31.8 1.6 constant_dynamic-slice_fusion.10
  33.4 1.7 constant_dynamic-slice_fusion.9
  35.0 1.8 constant_dynamic-slice_fusion.8
  36.8 1.8 constant_dynamic-slice_fusion.12
  38.5 2.1 constant_dynamic-slice_fusion.11
  40.6 2.8 constant_dynamic-slice_fusion.7
  43.4 2.3 constant_dynamic-slice_fusion.13
  45.8 64.2 %collective-permute-done.1.b_rcv = bf16[6144,6144]{1,0:T(8,128)(2,1)} collective-permute-done((bf16[6144,6144]{1,0:T(8,128)(2,1)}, bf16[6144,6144]{1,0:T(8,128)(2,1)}, u32[]{:S(2)}, u32[]{:S(2)}) %collective-permute-start.1) | collective-permute-done | bytes 75497504 | tf_op jit(solution)/shard_map/ppermute | solution.py:261
  109.9 2.8 collective-permute-start.10
  112.8 250.5 %shard_map.28.part_ref.refs_0_ = f32[3072,6144]{1,0:T(8,128)} custom-call(s32[2]{0:T(128)} %pad_add_fusion.meta_ref, bf16[6144,6144]{1,0:T(8,128)(2,1)} %a_ref.1, bf16[6144,6144]{1,0:T(8,128)(2,1)} %b_loc.25, bf16[6144,6144]{1,0:T(8,128)(2,1)} %collective-permute-done.1.b_rcv), custom_call_target="tpu_custom_call" | custom-call | flops 231928233984 | bytes 226492416 | tf_op jit(solution)/shard_map/pallas_call | solution.py:86
  363.3 8.4 %stage.1 = (bf16[1024,6144]{1,0:T(8,128)(2,1)S(1)}, f32[384,6144]{1,0:T(8,128)S(1)}, s32[2]{0:T(128)S(1)}) custom-call(s32[2]{0:T(128)S(1)} %copy-done, bf16[6144,6144]{1,0:T(8,128)(2,1)} %b_loc.25, bf16[6144,6144]{1,0:T(8,128)(2,1)} %collective-permute-done.1.b_rcv, f32[3072,6144]{1,0:T(8,128)} %shard_map.28.part_ref.refs_0_), custom_call_target="tpu_custom_call" | custom-call | flops 1000000000 | bytes 22020096 | tf_op jit(solution)/shard_map/stage/pallas_call | solution.py:191
  371.7 0.0 collective-permute-done.14.a_ref
  371.7 0.0 collective-permute-start.9
  371.8 29.2 %shard_map.33.refs_1_ = bf16[3072,6144]{1,0:T(8,128)(2,1)} custom-call(s32[2]{0:T(128)S(1)} %copy-done, bf16[32,6144]{1,0:T(8,128)(2,1)} %collective-permute-done.14.a_ref, bf16[6144,6144]{1,0:T(8,128)(2,1)} %b_loc.25, bf16[6144,6144]{1,0:T(8,128)(2,1)} %collective-permute-done.1.b_rcv, f32[3072,6144]{1,0:T(8,128)} %shard_map.28.part_ref.refs_0_), custom_call_target="tpu_custom_call" | custom-call | flops 2415919104 | bytes 77070336 | tf_op jit(solution)/shard_map/pallas_call | solution.py:86
  401.0 0.0 collective-permute-done.13.a_ref
  401.0 2.0 collective-permute-start.8
  403.0 29.7 %shard_map.34.refs_1_ = bf16[3072,6144]{1,0:T(8,128)(2,1)} custom-call(s32[2]{0:T(128)S(1)} %copy-done, bf16[96,6144]{1,0:T(8,128)(2,1)} %collective-permute-done.13.a_ref, bf16[6144,6144]{1,0:T(8,128)(2,1)} %b_loc.25, bf16[6144,6144]{1,0:T(8,128)(2,1)} %collective-permute-done.1.b_rcv, ...), custom_call_target="tpu_custom_call", output_to_operand_aliasing={{}: (5, {})} | custom-call | flops 7247757312 | bytes 80216064 | tf_op jit(solution)/shard_map/pallas_call | solution.py:86
  432.8 0.0 collective-permute-done.12.a_ref
  432.8 0.0 collective-permute-start.5
  432.8 48.6 %shard_map.35.refs_1_ = bf16[3072,6144]{1,0:T(8,128)(2,1)} custom-call(s32[2]{0:T(128)S(1)} %copy-done, bf16[512,6144]{1,0:T(8,128)(2,1)} %collective-permute-done.12.a_ref, bf16[6144,6144]{1,0:T(8,128)(2,1)} %b_loc.25, bf16[6144,6144]{1,0:T(8,128)(2,1)} %collective-permute-done.1.b_rcv, ...), custom_call_target="tpu_custom_call", output_to_operand_aliasing={{}: (5, {})} | custom-call | flops 38654705664 | bytes 100663296 | tf_op jit(solution)/shard_map/pallas_call | solution.py:86
  481.4 0.0 collective-permute-done.11.a_ref
  481.4 2.0 collective-permute-start.4
  483.5 48.6 %shard_map.36.refs_1_ = bf16[3072,6144]{1,0:T(8,128)(2,1)} custom-call(s32[2]{0:T(128)S(1)} %copy-done, bf16[512,6144]{1,0:T(8,128)(2,1)} %collective-permute-done.11.a_ref, bf16[6144,6144]{1,0:T(8,128)(2,1)} %b_loc.25, bf16[6144,6144]{1,0:T(8,128)(2,1)} %collective-permute-done.1.b_rcv, ...), custom_call_target="tpu_custom_call", output_to_operand_aliasing={{}: (5, {})} | custom-call | flops 38654705664 | bytes 100663296 | tf_op jit(solution)/shard_map/pallas_call | solution.py:86
  532.1 0.0 collective-permute-start.3
  532.1 48.6 %shard_map.37.refs_1_ = bf16[3072,6144]{1,0:T(8,128)(2,1)} custom-call(s32[2]{0:T(128)S(1)} %copy-done, bf16[512,6144]{1,0:T(8,128)(2,1)} %collective-permute-done.10.a_ref, bf16[6144,6144]{1,0:T(8,128)(2,1)} %b_loc.25, bf16[6144,6144]{1,0:T(8,128)(2,1)} %collective-permute-done.1.b_rcv, ...), custom_call_target="tpu_custom_call", output_to_operand_aliasing={{}: (5, {})} | custom-call | flops 38654705664 | bytes 100663296 | tf_op jit(solution)/shard_map/pallas_call | solution.py:86
  580.7 2.0 collective-permute-start.2
  582.7 48.8 %shard_map.38.refs_1_ = bf16[3072,6144]{1,0:T(8,128)(2,1)} custom-call(s32[2]{0:T(128)S(1)} %copy-done, bf16[512,6144]{1,0:T(8,128)(2,1)} %collective-permute-done.9.a_ref, bf16[6144,6144]{1,0:T(8,128)(2,1)} %b_loc.25, bf16[6144,6144]{1,0:T(8,128)(2,1)} %collective-permute-done.1.b_rcv, ...), custom_call_target="tpu_custom_call", output_to_operand_aliasing={{}: (5, {})} | custom-call | flops 38654705664 | bytes 100663296 | tf_op jit(solution)/shard_map/pallas_call | solution.py:86
  631.5 83.3 %collective-permute-done.8.a_ref = bf16[512,6144]{1,0:T(8,128)(2,1)} collective-permute-done((bf16[512,6144]{1,0:T(8,128)(2,1)}, bf16[512,6144]{1,0:T(8,128)(2,1)}, u32[]{:S(2)}, u32[]{:S(2)}) %collective-permute-start.8) | collective-permute-done | bytes 6291488 | tf_op jit(solution)/shard_map/ppermute | solution.py:260
  714.8 2.0 collective-permute-start.7
  716.8 48.6 %shard_map.39._ = bf16[3072,6144]{1,0:T(8,128)(2,1)} custom-call(s32[2]{0:T(128)S(1)} %get-tuple-element.9.meta_ref, bf16[512,6144]{1,0:T(8,128)(2,1)} %collective-permute-done.8.a_ref, bf16[6144,6144]{1,0:T(8,128)(2,1)} %b_loc.25, bf16[6144,6144]{1,0:T(8,128)(2,1)} %collective-permute-done.1.b_rcv, ...), custom_call_target="tpu_custom_call", output_to_operand_aliasing={{}: (5, {})} | custom-call | flops 38654705664 | bytes 100663296 | tf_op jit(solution)/shard_map/pallas_call | solution.py:86
  765.4 0.0 collective-permute-start.6
  765.4 14.4 %shard_map.29.acc_in = f32[384,6144]{1,0:T(8,128)S(1)} custom-call(s32[2]{0:T(128)S(1)} %get-tuple-element.9.meta_ref, bf16[384,2048]{1,0:T(8,128)(2,1)} %collective-permute-done.5.a_ref, bf16[6144,6144]{1,0:T(8,128)(2,1)} %b_loc.25, bf16[6144,6144]{1,0:T(8,128)(2,1)} %collective-permute-done.1.b_rcv, ...), custom_call_target="tpu_custom_call", output_to_operand_aliasing={{}: (4, {})} | custom-call | flops 9663676416 | bytes 25165824 | tf_op jit(solution)/shard_map/pallas_call | solution.py:207
  779.9 2.0 collective-permute-start
  781.9 11.7 %shard_map.30.acc_in = f32[384,6144]{1,0:T(8,128)S(1)} custom-call(s32[2]{0:T(128)S(1)} %get-tuple-element.9.meta_ref, bf16[384,1536]{1,0:T(8,128)(2,1)} %collective-permute-done.4.a_ref, bf16[6144,6144]{1,0:T(8,128)(2,1)} %b_loc.25, bf16[6144,6144]{1,0:T(8,128)(2,1)} %collective-permute-done.1.b_rcv, ...), custom_call_target="tpu_custom_call", output_to_operand_aliasing={{}: (4, {})} | custom-call | flops 7247757312 | bytes 18874368 | tf_op jit(solution)/shard_map/pallas_call | solution.py:207
  793.6 8.7 %shard_map.31.acc_in = f32[384,6144]{1,0:T(8,128)S(1)} custom-call(s32[2]{0:T(128)S(1)} %get-tuple-element.9.meta_ref, bf16[384,1024]{1,0:T(8,128)(2,1)} %collective-permute-done.3.a_ref, bf16[6144,6144]{1,0:T(8,128)(2,1)} %b_loc.25, bf16[6144,6144]{1,0:T(8,128)(2,1)} %collective-permute-done.1.b_rcv, ...), custom_call_target="tpu_custom_call", output_to_operand_aliasing={{}: (4, {})} | custom-call | flops 4831838208 | bytes 12582912 | tf_op jit(solution)/shard_map/pallas_call | solution.py:207
  802.3 6.1 shard_map.32.acc_ref
  808.4 4.1 shard_map.40._
  812.6 3.6 shard_map.41._
  816.2 3.7 shard_map.42
  (11 shorter events, 0.0 us)
Async XLA Ops:
  0.0 109.9 %collective-permute-start.1 = (bf16[6144,6144]{1,0:T(8,128)(2,1)}, bf16[6144,6144]{1,0:T(8,128)(2,1)}, u32[]{:S(2)}, u32[]{:S(2)}) collective-permute-start(bf16[6144,6144]{1,0:T(8,128)(2,1)} %b_loc.25), channel_id=1, source_target_pairs={{0,1},{1,0},{2,3},{3,2},{4,5},{5,4},{6,7},{7,6}} | collective-permute-start | bytes 226492416 | tf_op jit(solution)/shard_map/ppermute | solution.py:261
  2.6 369.1 %collective-permute-start.14 = (bf16[32,6144]{1,0:T(8,128)(2,1)}, bf16[32,6144]{1,0:T(8,128)(2,1)}, u32[]{:S(2)}, u32[]{:S(2)}) collective-permute-start(bf16[32,6144]{1,0:T(8,128)(2,1)} %constant_dynamic-slice_fusion), channel_id=1, source_target_pairs={{0,2},{2,0},{1,3},{3,1},{4,6},{6,4},{5,7},{7,5}} | collective-permute-start | bytes 1179656 | tf_op jit(solution)/shard_map/ppermute | solution.py:260
  7.4 393.6 %collective-permute-start.13 = (bf16[96,6144]{1,0:T(8,128)(2,1)}, bf16[96,6144]{1,0:T(8,128)(2,1)}, u32[]{:S(2)}, u32[]{:S(2)}) collective-permute-start(bf16[96,6144]{1,0:T(8,128)(2,1)} %constant_dynamic-slice_fusion.1), channel_id=1, source_target_pairs={{0,2},{2,0},{1,3},{3,1},{4,6},{6,4},{5,7},{7,5}} | collective-permute-start | bytes 3538952 | tf_op jit(solution)/shard_map/ppermute | solution.py:260
  29.1 403.7 %collective-permute-start.12 = (bf16[512,6144]{1,0:T(8,128)(2,1)}, bf16[512,6144]{1,0:T(8,128)(2,1)}, u32[]{:S(2)}, u32[]{:S(2)}) collective-permute-start(bf16[512,6144]{1,0:T(8,128)(2,1)} %get-tuple-element.11), channel_id=1, source_target_pairs={{0,2},{2,0},{1,3},{3,1},{4,6},{6,4},{5,7},{7,5}} | collective-permute-start | bytes 18874376 | tf_op jit(solution)/shard_map/ppermute | solution.py:260
  31.1 450.3 %collective-permute-start.11 = (bf16[512,6144]{1,0:T(8,128)(2,1)}, bf16[512,6144]{1,0:T(8,128)(2,1)}, u32[]{:S(2)}, u32[]{:S(2)}) collective-permute-start(bf16[512,6144]{1,0:T(8,128)(2,1)} %get-tuple-element.12), channel_id=1, source_target_pairs={{0,2},{2,0},{1,3},{3,1},{4,6},{6,4},{5,7},{7,5}} | collective-permute-start | bytes 18874376 | tf_op jit(solution)/shard_map/ppermute | solution.py:260
  109.9 422.1 %collective-permute-start.10 = (bf16[512,6144]{1,0:T(8,128)(2,1)}, bf16[512,6144]{1,0:T(8,128)(2,1)}, u32[]{:S(2)}, u32[]{:S(2)}) collective-permute-start(bf16[512,6144]{1,0:T(8,128)(2,1)} %get-tuple-element.13), channel_id=1, source_target_pairs={{0,2},{2,0},{1,3},{3,1},{4,6},{6,4},{5,7},{7,5}} | collective-permute-start | bytes 18874376 | tf_op jit(solution)/shard_map/ppermute | solution.py:260
  112.8 250.5 %copy-start = (s32[2]{0:T(128)S(1)}, s32[2]{0:T(128)}, u32[]{:S(2)}) copy-start(s32[2]{0:T(128)} %pad_add_fusion.meta_ref) | copy-start | bytes 28
  371.7 209.0 %collective-permute-start.9 = (bf16[512,6144]{1,0:T(8,128)(2,1)}, bf16[512,6144]{1,0:T(8,128)(2,1)}, u32[]{:S(2)}, u32[]{:S(2)}) collective-permute-start(bf16[512,6144]{1,0:T(8,128)(2,1)} %get-tuple-element.14), channel_id=1, source_target_pairs={{0,2},{2,0},{1,3},{3,1},{4,6},{6,4},{5,7},{7,5}} | collective-permute-start | bytes 18874376 | tf_op jit(solution)/shard_map/ppermute | solution.py:260
  401.0 313.8 %collective-permute-start.8 = (bf16[512,6144]{1,0:T(8,128)(2,1)}, bf16[512,6144]{1,0:T(8,128)(2,1)}, u32[]{:S(2)}, u32[]{:S(2)}) collective-permute-start(bf16[512,6144]{1,0:T(8,128)(2,1)} %get-tuple-element.15), channel_id=1, source_target_pairs={{0,2},{2,0},{1,3},{3,1},{4,6},{6,4},{5,7},{7,5}} | collective-permute-start | bytes 18874376 | tf_op jit(solution)/shard_map/ppermute | solution.py:260
  432.8 332.6 %collective-permute-start.5 = (bf16[384,2048]{1,0:T(8,128)(2,1)}, bf16[384,2048]{1,0:T(8,128)(2,1)}, u32[]{:S(2)}, u32[]{:S(2)}) collective-permute-start(bf16[384,2048]{1,0:T(8,128)(2,1)} %constant_dynamic-slice_fusion.7), channel_id=1, source_target_pairs={{0,2},{2,0},{1,3},{3,1},{4,6},{6,4},{5,7},{7,5}} | collective-permute-start | bytes 4718600 | tf_op jit(solution)/shard_map/ppermute | solution.py:260
  481.4 298.4 %collective-permute-start.4 = (bf16[384,1536]{1,0:T(8,128)(2,1)}, bf16[384,1536]{1,0:T(8,128)(2,1)}, u32[]{:S(2)}, u32[]{:S(2)}) collective-permute-start(bf16[384,1536]{1,0:T(8,128)(2,1)} %constant_dynamic-slice_fusion.13), channel_id=1, source_target_pairs={{0,2},{2,0},{1,3},{3,1},{4,6},{6,4},{5,7},{7,5}} | collective-permute-start | bytes 3538952 | tf_op jit(solution)/shard_map/ppermute | solution.py:260
  532.1 261.6 %collective-permute-start.3 = (bf16[384,1024]{1,0:T(8,128)(2,1)}, bf16[384,1024]{1,0:T(8,128)(2,1)}, u32[]{:S(2)}, u32[]{:S(2)}) collective-permute-start(bf16[384,1024]{1,0:T(8,128)(2,1)} %constant_dynamic-slice_fusion.11), channel_id=1, source_target_pairs={{0,2},{2,0},{1,3},{3,1},{4,6},{6,4},{5,7},{7,5}} | collective-permute-start | bytes 2359304 | tf_op jit(solution)/shard_map/ppermute | solution.py:260
  580.7 221.6 %collective-permute-start.2 = (bf16[384,512]{1,0:T(8,128)(2,1)}, bf16[384,512]{1,0:T(8,128)(2,1)}, u32[]{:S(2)}, u32[]{:S(2)}) collective-permute-start(bf16[384,512]{1,0:T(8,128)(2,1)} %constant_dynamic-slice_fusion.12), channel_id=1, source_target_pairs={{0,2},{2,0},{1,3},{3,1},{4,6},{6,4},{5,7},{7,5}} | collective-permute-start | bytes 1179656 | tf_op jit(solution)/shard_map/ppermute | solution.py:260
  714.8 93.7 %collective-permute-start.7 = (bf16[176,1024]{1,0:T(8,128)(2,1)}, bf16[176,1024]{1,0:T(8,128)(2,1)}, u32[]{:S(2)}, u32[]{:S(2)}) collective-permute-start(bf16[176,1024]{1,0:T(8,128)(2,1)} %constant_dynamic-slice_fusion.8), channel_id=1, source_target_pairs={{0,2},{2,0},{1,3},{3,1},{4,6},{6,4},{5,7},{7,5}} | collective-permute-start | bytes 1081352 | tf_op jit(solution)/shard_map/ppermute | solution.py:260
  765.4 47.2 %collective-permute-start.6 = (bf16[112,1024]{1,0:T(8,128)(2,1)}, bf16[112,1024]{1,0:T(8,128)(2,1)}, u32[]{:S(2)}, u32[]{:S(2)}) collective-permute-start(bf16[112,1024]{1,0:T(8,128)(2,1)} %constant_dynamic-slice_fusion.9), channel_id=1, source_target_pairs={{0,2},{2,0},{1,3},{3,1},{4,6},{6,4},{5,7},{7,5}} | collective-permute-start | bytes 688136 | tf_op jit(solution)/shard_map/ppermute | solution.py:260
  779.9 36.3 %collective-permute-start = (bf16[96,1024]{1,0:T(8,128)(2,1)}, bf16[96,1024]{1,0:T(8,128)(2,1)}, u32[]{:S(2)}, u32[]{:S(2)}) collective-permute-start(bf16[96,1024]{1,0:T(8,128)(2,1)} %constant_dynamic-slice_fusion.10), channel_id=1, source_target_pairs={{0,2},{2,0},{1,3},{3,1},{4,6},{6,4},{5,7},{7,5}} | collective-permute-start | bytes 589832 | tf_op jit(solution)/shard_map/ppermute | solution.py:260
